TPU v7x, 256 devices: a whole 4x4x8 slice. The times are simulated.
256 devices in a mesh: ep: 64 (over x, z, core), dp: 4 (over y).
Axes of the slice: x: 4, y: 4, z: 8, core: 2. Of those that a mesh axis runs over, the one named last changes fastest.
Arguments:
- tokens: bfloat16 [32768, 2048], P(('ep', 'dp')), may hold values from -6 to 6
- routes: int32 [32768, 8], P(('ep', 'dp')), may hold values from 0 to 63, as said below
- gates: bfloat16 [32768, 8], P(('ep', 'dp')), may hold values from 0.19921875 to 1
- w_gate: bfloat16 [64, 2048, 768], P('ep'), may hold values from -0.125 to 0.125
- w_up: bfloat16 [64, 2048, 768], P('ep'), may hold values from -0.125 to 0.125
- w_down: bfloat16 [64, 768, 2048], P('ep'), may hold values from -0.21875 to 0.21875
- score_head: float32 [2048], replicated, may hold values from -0.125 to 0.125
- doc_ids: int32 [256], P(('ep', 'dp')), may hold values from 0 to 63, never falling along the last dimension, each value on 1 to 8 neighbouring positions
Outputs:
- mixed: bfloat16 [32768, 2048], P(('ep', 'dp'))
- doc_scores: float32 [3, 64], replicated
Inputs may be any that keep to these rules, and one draw needn't show every extreme that they name: `routes`: each row names 8 different experts; among the rows of one device no expert is named more than 24 times. `doc_ids`: never falling along the passages; every document has 1 to 8 passages.
All inputs are finite; a program needn't handle non-finite values.
Results may differ from a plain program's by a relative error of at most 0.0058.
Values may be sent and summed in bfloat16 or wider, within the bound.
A program may use at most 64 MiB of HBM per device.

v0:
```python
import math

import jax
import jax.numpy as jnp
from jax import lax
from jax.sharding import Mesh
from jax.sharding import PartitionSpec as P

TOP = 8
PASSAGE = 128
EP = ("ep_0", "ep_1", "ep_2")
EP_DP = ("ep_0", "ep_1", "ep_2", "dp")


far_index = 1000000000.0


def sent_together(arrays, axis, split_dim, concat_dim, along):
    columns = [a.reshape(*a.shape[:along], -1) for a in arrays]
    both = jnp.concatenate(columns, axis=along)
    filled, at, done = (
        lax.all_to_all(both, axis, split_axis=split_dim, concat_axis=concat_dim, tiled=True),
        0,
        [],
    )
    for a, column in zip(arrays, columns):
        section = filled[..., at : at + column.shape[along]]
        done.append(section.reshape(*section.shape[:along], *a.shape[along:]))
        at += column.shape[along]
    return tuple(done)


def all_in_one(shard, axis):
    leaves = jax.tree.leaves(shard)
    order = sorted(range(len(leaves)), key=lambda k: -leaves[k].size)
    width = (1, *leaves[order[0]].shape)[-1]
    lines = [
        jnp.pad(leaves[k].reshape(-1), (0, -leaves[k].size % width)).reshape(-1, width)
        for k in order
    ]
    both, at, found = (lax.all_gather(jnp.concatenate(lines), axis), 0, {})
    for k, line in zip(order, lines):
        section = both[:, at : at + len(line)].reshape(len(both), -1)
        found[k] = section[:, : leaves[k].size].reshape(-1, *leaves[k].shape)
        at += len(line)
    numbers = iter(range(len(leaves)))
    return jax.tree.map(lambda _: found[next(numbers)], shard)


def combined_by_axis(shard, axes, combine):
    for axis in axes:
        pieces = all_in_one(shard, axis)
        shard = jax.tree.map(lambda part: part[0], pieces)
        for k in range(1, lax.axis_size(axis)):
            shard = combine(shard, jax.tree.map(lambda part: part[k], pieces))
    return shard


def expert_rows(rows, gate_rows, wg_single, wu_single, wd_single):
    gate_part = jnp.dot(rows, wg_single, preferred_element_type=jnp.float32)
    up_part = jnp.dot(rows, wu_single, preferred_element_type=jnp.float32)
    hidden = (jax.nn.silu(gate_part) * up_part).astype(jnp.bfloat16)
    result = jnp.dot(hidden, wd_single, preferred_element_type=jnp.float32)
    return (gate_rows.astype(jnp.float32)[:, None] * result).astype(jnp.bfloat16)


def run_expert(slot_rows, slot_gates, wg_single, wu_single, wd_single):
    width = slot_rows.shape[-1]
    rows = slot_rows.reshape(-1, width)
    gate_rows = slot_gates.reshape(-1)
    result = expert_rows(rows, gate_rows, wg_single, wu_single, wd_single)
    return result.reshape(slot_rows.shape)


def shards(tokens, routes, gates, w_gate, w_up, w_down, score_head, doc_ids):
    tok_dev, width = tokens.shape
    experts = lax.axis_size(EP)
    capacity = min(tok_dev, 3 * tok_dev * TOP // (2 * experts))
    flat_routes = routes.reshape(-1)
    onehot = (flat_routes[:, None] == jnp.arange(experts, dtype=jnp.int32)[None, :]).astype(
        jnp.int32
    )
    ranked = jnp.cumsum(onehot, axis=0)
    slot = jnp.sum(ranked * onehot, axis=1) - 1
    destination = flat_routes * capacity + slot
    repeated = jnp.repeat(tokens, TOP, axis=0)
    send_rows = jnp.zeros((experts * capacity, width), jnp.bfloat16).at[destination].set(repeated)
    send_gates = (
        jnp.zeros((experts * capacity,), jnp.bfloat16).at[destination].set(gates.reshape(-1))
    )
    recv_rows, recv_gates = sent_together(
        (send_rows.reshape(experts, capacity, width), send_gates.reshape(experts, capacity)),
        EP,
        0,
        0,
        2,
    )
    wg_single = w_gate[0]
    wu_single = w_up[0]
    wd_single = w_down[0]
    results = run_expert(recv_rows, recv_gates, wg_single, wu_single, wd_single)
    returned = lax.all_to_all(results, EP, split_axis=0, concat_axis=0, tiled=True)
    returned_flat = returned.reshape(experts * capacity, width)
    gathered = returned_flat[destination].astype(jnp.float32).reshape(tok_dev, TOP, width)
    mixed = jnp.sum(gathered, axis=1).astype(jnp.bfloat16)
    token_score = jnp.dot(mixed.astype(jnp.float32), score_head, precision=lax.Precision.HIGHEST)
    passage_score = token_score.reshape(-1, PASSAGE).sum(axis=1) / math.sqrt(PASSAGE)
    local_passages = passage_score.shape[0]
    doc_count = lax.axis_size(EP) * lax.axis_size("dp") * tok_dev // PASSAGE // 4
    doc_range = jnp.arange(doc_count, dtype=jnp.int32)[None, :]
    member = doc_ids[:, None] == doc_range
    column = passage_score[:, None]
    device_index = lax.axis_index(EP_DP)
    global_index = (
        device_index * local_passages + jnp.arange(local_passages, dtype=jnp.int32)
    ).astype(jnp.float32)[:, None]
    part_max = jnp.where(member, column, -1e30).max(axis=0)
    part_sum = jnp.where(member, column, 0.0).sum(axis=0)
    part_first = jnp.where(member, global_index, far_index).min(axis=0)
    part_value = jnp.where(member & (global_index == part_first[None, :]), column, 0.0).sum(axis=0)

    def combine(left, right):
        earlier = left[2] <= right[2]
        return (
            jnp.maximum(left[0], right[0]),
            left[1] + right[1],
            jnp.minimum(left[2], right[2]),
            jnp.where(earlier, left[3], right[3]),
        )

    max_score, sum_score, _, first_score = combined_by_axis(
        (part_max, part_sum, part_first, part_value), EP_DP, combine
    )
    return (mixed, jnp.stack([max_score, first_score, sum_score]))


def solution(mesh):
    finer = Mesh(mesh.devices.reshape(4, 8, 2, mesh.shape["dp"]), ("ep_0", "ep_1", "ep_2", "dp"))
    return jax.shard_map(
        shards,
        mesh=finer,
        in_specs=(
            P(EP_DP, None),
            P(EP_DP, None),
            P(EP_DP, None),
            P(EP, None, None),
            P(EP, None, None),
            P(EP, None, None),
            P(),
            P(EP_DP),
        ),
        out_specs=(P(EP_DP, None), P()),
        check_vma=False,
    )
```

profile of v0, /device:TPU:1, one launch (start us, length us, event | category | flops | bytes accessed | tf_op | source)
XLA Modules:
  0.0 457.9 jit_solution(18129349465002221860)
XLA Ops:
  0.6 0.0 copy-start
  0.6 0.8 broadcast_multiply_fusion
  1.5 0.9 copy.25
  2.4 0.1 eq.77
  2.5 0.1 eq.73
  2.6 0.8 copy.29
  3.4 0.1 reshape.1271
  3.5 0.1 copy.24
  3.6 0.1 mul.45
  3.7 0.7 fusion.11
  4.4 31.1 %reduce-window.6 = s32[64,8,128]{2,1,0:T(8,128)S(1)} reduce-window(s32[64,8,128]{2,1,0:T(8,128)} %fusion.11, s32[]{:T(128)} %constant.20.clone.1), window={size=1x1x128 pad=0_0x0_0x127_0}, to_apply=%region_0.0 | reduce-window | flops 8323072 | bytes 524292 | tf_op jit(solution)/shard_map/reduce-window
  35.5 0.8 slice.466
  36.3 1.1 copy.27
  37.5 0.1 copy.28
  37.5 0.1 broadcast_add_fusion
  37.7 0.1 fusion.10
  37.8 7.6 %scatter_custom_fusion.1 = bf16[1536]{0:T(1024)(128)(2,1)S(1)} fusion(s32[1024]{0:T(1024)S(1)} %bitcast.93, bf16[1024]{0:T(1024)(128)(2,1)S(1)} %reshape.1271, bf16[]{:T(256)} %constant.18.clone.1), kind=kCustom, calls=%fused_computation.32 | custom fusion | bytes 3074 | tf_op jit(solution)/shard_map/scatter | solution.py:89
  45.4 0.7 reshape_reshape.5
  46.1 10.7 %scatter_custom_fusion = bf16[1536,2048]{1,0:T(8,128)(2,1)} fusion(s32[1024]{0:T(1024)S(1)} %bitcast.94, bf16[]{:T(256)} %constant.18.clone.1, bf16[128,2048]{1,0:T(8,128)(2,1)} %param.8), kind=kCustom, calls=%fused_computation.7 | custom fusion | bytes 6815746 | tf_op jit(solution)/shard_map/scatter | solution.py:87
  56.7 3.5 pad_maximum_fusion
  60.2 162.1 %all_to_all.10 = bf16[64,24,2049]{2,1,0:T(8,128)(2,1)S(1)} all-to-all(bf16[64,24,2049]{2,1,0:T(8,128)(2,1)S(1)} %pad_maximum_fusion), channel_id=1, replica_groups=mesh['ep_0'=4,'ep_1'=8,'ep_2'=2,'dp'=4] {'ep_0','ep_1','ep_2'}, dimensions={0} | all-to-all | bytes 12589056 | tf_op jit(solution)/shard_map/all_to_all | solution.py:22
  222.4 0.0 copy-start.1
  222.4 2.8 copy-done.1
  225.2 0.3 convert_reduce_fusion
  225.4 0.1 reshape.1234
  225.5 0.0 copy-start.4
  225.5 3.5 slice.469
  229.1 0.2 copy-done.4
  229.2 0.0 copy-start.5
  229.2 5.3 %fusion.4 = f32[1536,768]{1,0:T(8,128)S(1)} fusion(bf16[1536,2048]{1,0:T(8,128)(2,1)S(1)} %bitcast.89, bf16[1,2048,768]{2,1,0:T(8,128)(2,1)S(1)} %copy-done.4), kind=kOutput, calls=%fused_computation.11 | convolution fusion | flops 4831838208 | bytes 14155776 | tf_op jit(solution)/shard_map/dot_general | solution.py:60
  234.5 0.0 copy-done.5
  234.5 5.7 %multiply_convert_fusion.1 = bf16[1536,768]{1,0:T(8,128)(2,1)S(1)} fusion(f32[1536,768]{1,0:T(8,128)S(1)} %fusion.4, bf16[1536,2048]{1,0:T(8,128)(2,1)S(1)} %bitcast.90, bf16[1,2048,768]{2,1,0:T(8,128)(2,1)S(1)} %copy-done.5), kind=kOutput, calls=%fused_computation.5 | convolution fusion | flops 4838916096 | bytes 16515072 | tf_op jit(solution)/shard_map/dot_general | solution.py:61
  240.2 0.0 copy-done
  240.2 7.1 %multiply_convert_fusion = bf16[1536,2048]{1,0:T(8,128)(2,1)} fusion(bf16[1536,768]{1,0:T(8,128)(2,1)S(1)} %multiply_convert_fusion.1, f32[1536]{0:T(1024)S(1)} %reshape.1234, bf16[1,768,2048]{2,1,0:T(8,128)(2,1)S(1)} %copy-done), kind=kOutput, calls=%fused_computation.3 | convolution fusion | flops 4838129664 | bytes 11802624 | tf_op jit(solution)/shard_map/dot_general | solution.py:63
  247.3 6.4 %all-to-all-start.1 = ((bf16[64,24,2048]{2,1,0:T(8,128)(2,1)}), bf16[64,24,2048]{2,1,0:T(8,128)(2,1)}, u32[]{:S(2)}, u32[]{:S(2)}) async-start(bf16[64,24,2048]{2,1,0:T(8,128)(2,1)} %bitcast.88), calls=%async_computation.1 | async-start | bytes 12582912 | tf_op jit(solution)/shard_map/all_to_all | solution.py:102
  254.4 140.1 %all-to-all-done.1 = bf16[64,24,2048]{2,1,0:T(8,128)(2,1)} async-done(((bf16[64,24,2048]{2,1,0:T(8,128)(2,1)}), bf16[64,24,2048]{2,1,0:T(8,128)(2,1)}, u32[]{:S(2)}, u32[]{:S(2)}) %all-to-all-start.1) | async-done | bytes 6291488 | tf_op jit(solution)/shard_map/all_to_all | solution.py:102
  394.5 12.4 %gather_fusion = bf16[1024,2048]{1,0:T(8,128)(2,1)} fusion(bf16[1536,2048]{1,0:T(8,128)(2,1)} %bitcast.11, s32[1024]{0:T(1024)S(1)} %broadcast_clamp_fusion), kind=kCustom, calls=%fused_computation | custom fusion | bytes 8392704 | tf_op jit(solution)/shard_map/gather | solution.py:104
  406.9 0.0 copy-start.3
  406.9 5.1 %bitcast_reduce_fusion = bf16[128,2048]{1,0:T(8,128)(2,1)S(1)} fusion(bf16[1024,2048]{1,0:T(8,128)(2,1)} %gather_fusion), kind=kLoop, calls=%fused_computation.6 | loop fusion | flops 1835008 | bytes 4718592 | tf_op jit(solution)/shard_map/reduce_sum | solution.py:105
  412.0 0.0 copy-start.2
  412.0 0.8 copy-done.2
  412.8 0.0 copy-done.3
  412.8 1.1 fusion.8
  414.6 8.5 %all-gather.4 = f32[4,4,64]{2,1,0:T(4,128)S(1)} all-gather(f32[1,4,64]{2,1,0:T(4,128)S(1)} %maximum_bitcast_fusion), channel_id=2, replica_groups=mesh['ep_0'=4,'ep_1'=8,'ep_2'=2,'dp'=4] {'ep_0'}, dimensions={0}, use_global_device_ids=true | all-gather | bytes 5120 | tf_op jit(solution)/shard_map/all_gather | solution.py:41
  423.2 15.6 %all-gather.5 = f32[8,4,64]{2,1,0:T(4,128)S(1)} all-gather(f32[1,4,64]{2,1,0:T(4,128)S(1)} %maximum_bitcast_fusion.1), channel_id=3, replica_groups=mesh['ep_0'=4,'ep_1'=8,'ep_2'=2,'dp'=4] {'ep_1'}, dimensions={0}, use_global_device_ids=true | all-gather | bytes 9216 | tf_op jit(solution)/shard_map/all_gather | solution.py:41
  438.9 9.7 %all-gather.6 = f32[2,4,64]{2,1,0:T(4,128)S(1)} all-gather(f32[1,4,64]{2,1,0:T(4,128)S(1)} %maximum_bitcast_fusion.2), channel_id=4, replica_groups=mesh['ep_0'=4,'ep_1'=8,'ep_2'=2,'dp'=4] {'ep_2'}, dimensions={0}, use_global_device_ids=true | all-gather | bytes 3072 | tf_op jit(solution)/shard_map/all_gather | solution.py:41
  448.6 8.7 %all-gather.7 = f32[4,4,64]{2,1,0:T(4,128)S(1)} all-gather(f32[1,4,64]{2,1,0:T(4,128)S(1)} %maximum_bitcast_fusion.3), channel_id=5, replica_groups=mesh['ep_0'=4,'ep_1'=8,'ep_2'=2,'dp'=4] {'dp'}, dimensions={0}, use_global_device_ids=true | all-gather | bytes 5120 | tf_op jit(solution)/shard_map/all_gather | solution.py:41
  457.3 0.6 pad_maximum_fusion.1
  (18 shorter events, 0.2 us)
Async XLA Ops:
  0.6 239.5 %copy-start = (bf16[1,768,2048]{2,1,0:T(8,128)(2,1)S(1)}, bf16[1,768,2048]{2,1,0:T(8,128)(2,1)}, u32[]{:S(2)}) copy-start(bf16[1,768,2048]{2,1,0:T(8,128)(2,1)} %param.13) | copy-start | bytes 9437188
  222.4 2.8 copy-start.1
  225.5 3.7 copy-start.4
  229.2 5.3 %copy-start.5 = (bf16[1,2048,768]{2,1,0:T(8,128)(2,1)S(1)}, bf16[1,2048,768]{2,1,0:T(8,128)(2,1)}, u32[]{:S(2)}) copy-start(bf16[1,2048,768]{2,1,0:T(8,128)(2,1)} %param.12) | copy-start | bytes 9437188
  247.3 147.2 %all-to-all-start.1 = ((bf16[64,24,2048]{2,1,0:T(8,128)(2,1)}), bf16[64,24,2048]{2,1,0:T(8,128)(2,1)}, u32[]{:S(2)}, u32[]{:S(2)}) async-start(bf16[64,24,2048]{2,1,0:T(8,128)(2,1)} %bitcast.88), calls=%async_computation.1 | async-start | bytes 12582912 | tf_op jit(solution)/shard_map/all_to_all | solution.py:102
  406.9 5.9 %copy-start.3 = (f32[2048]{0:T(1024)S(1)}, f32[2048]{0:T(1024)}, u32[]{:S(2)}) copy-start(f32[2048]{0:T(1024)} %param.14) | copy-start | bytes 24580
  412.0 0.8 copy-start.2
where the time goes:
time: 461 us; the launch traced here: 458 us
  blocking collectives  205 us (44%)
  waiting for transfers between devices  140 us (30%)
  local copies, waits for them, and re-layouts  42.9 us (9%)
  other arithmetic  42.5 us (9%)
  matrix products  19.1 us (4%)
  starting transfers between devices  6.43 us (1%)
    all_to_all x1, blocking collectives, sent_together(): lax.all_to_all(both, axis, split_axis=split_dim, concat_axis=concat_dim,...  162 us
    all_to_all x1, waiting for transfers between devices, shards(): lax.all_to_all(results, EP, split_axis=0, concat_axis=0, tiled=True)  140 us
    all_gather x4, blocking collectives, all_in_one(): both, at, found = (lax.all_gather(jnp.concatenate(lines), axis), 0, {})  42.5 us
    another operation x3, other arithmetic  31.3 us
    gather x1, local copies, waits for them, and re-layouts, shards(): returned_flat[destination].astype(jnp.float32).reshape(tok_dev, TOP, width)  12.4 us
    scatter x1, local copies, waits for them, and re-layouts, shards(): jnp.zeros((experts * capacity, width), jnp.bfloat16).at[destination]  10.7 us
  transfers between devices with their start and end apart: 1, of which 1 were waited for; matrix products, arithmetic and copies ran while one was open for 0% of the time, Pallas kernels for 0%

commit v1 on v0

v1 whole, which is shorter than its diff:
```python
import math

import jax
import jax.numpy as jnp
from jax import lax
from jax.sharding import Mesh
from jax.sharding import PartitionSpec as P

TOP = 8
PASSAGE = 128
EP = ("x", "z", "core")
EP_DP = ("x", "z", "core", "dp")
CAP = 24


def shards(tokens, routes, gates, w_gate, w_up, w_down, score_head, doc_ids):
    rows, width = tokens.shape
    nx, nz, nc = lax.axis_size("x"), lax.axis_size("z"), lax.axis_size("core")
    experts = nx * nz * nc
    hit = routes[:, :, None] == jnp.arange(experts, dtype=jnp.int32)
    routed = hit.any(axis=1)
    gate_of = jnp.where(hit, gates[:, :, None], 0).sum(axis=1)
    below = jnp.tril(jnp.ones((rows, rows), jnp.bfloat16), -1)
    rank = jnp.dot(below, routed.astype(jnp.bfloat16), preferred_element_type=jnp.float32)
    rank = jnp.where(routed, rank, 200.0).astype(jnp.bfloat16)
    packed = jnp.concatenate([tokens, rank, gate_of.astype(jnp.bfloat16)], axis=1)
    held = lax.all_gather(packed, "z")
    mine = lax.axis_index("z")

    def at_z(a):
        a = a.reshape(nz, rows, nx, nz, nc)
        return lax.dynamic_index_in_dim(a, mine, 3, keepdims=False).reshape(nz, rows, nx * nc)

    rank_z = at_z(held[..., width : width + experts])
    gate_z = at_z(held[..., width + experts :])
    slots = jnp.arange(CAP, dtype=jnp.bfloat16)
    chosen = rank_z.transpose(2, 0, 1)[:, :, None, :] == slots[:, None]
    pick = chosen.astype(jnp.bfloat16)
    send = jnp.einsum("dslt,stf->dslf", pick, held[..., :width], preferred_element_type=jnp.bfloat16)
    send = send.reshape(nx * nc, nz * CAP, width)
    recv = lax.all_to_all(send, ("x", "core"), split_axis=0, concat_axis=0, tiled=True)
    flat = recv.reshape(-1, width)
    gate_part = jnp.dot(flat, w_gate[0], preferred_element_type=jnp.float32)
    up_part = jnp.dot(flat, w_up[0], preferred_element_type=jnp.float32)
    hidden = (jax.nn.silu(gate_part) * up_part).astype(jnp.bfloat16)
    result = jnp.dot(hidden, w_down[0], preferred_element_type=jnp.float32).astype(jnp.bfloat16)
    back = lax.all_to_all(
        result.reshape(recv.shape), ("x", "core"), split_axis=0, concat_axis=0, tiled=True
    ).reshape(nx * nc, nz, CAP, width)
    mix = jnp.where(chosen, gate_z.transpose(2, 0, 1)[:, :, None, :], 0)
    part = jnp.einsum("dslt,dslf->stf", mix, back, preferred_element_type=jnp.float32)
    mixed = lax.psum_scatter(part.astype(jnp.bfloat16), "z", scatter_dimension=0, tiled=False)

    token_score = jnp.dot(mixed.astype(jnp.float32), score_head, precision=lax.Precision.HIGHEST)
    passage_score = token_score.reshape(-1, PASSAGE).sum(axis=1) / math.sqrt(PASSAGE)
    pair = jnp.stack([passage_score, doc_ids.astype(jnp.float32)], axis=1)
    pairs = lax.all_gather(pair, EP_DP, tiled=True)
    total = pairs.shape[0]
    docs = total // 4
    column = pairs[:, :1]
    member = pairs[:, 1:] == jnp.arange(docs, dtype=jnp.float32)[None, :]
    index = jnp.arange(total, dtype=jnp.int32)[:, None]
    max_score = jnp.where(member, column, -1e30).max(axis=0)
    sum_score = jnp.where(member, column, 0.0).sum(axis=0)
    first = jnp.where(member, index, total).min(axis=0)
    first_score = jnp.where(member & (index == first[None, :]), column, 0.0).sum(axis=0)
    return mixed, jnp.stack([max_score, first_score, sum_score])


def solution(mesh):
    finer = Mesh(mesh.devices.reshape(4, 8, 2, mesh.shape["dp"]), EP_DP)
    return jax.shard_map(
        shards,
        mesh=finer,
        in_specs=(
            P(EP_DP, None),
            P(EP_DP, None),
            P(EP_DP, None),
            P(EP, None, None),
            P(EP, None, None),
            P(EP, None, None),
            P(),
            P(EP_DP),
        ),
        out_specs=(P(EP_DP, None), P()),
        check_vma=False,
    )
```

time: 461 us -> 413 us (0.90)
  waiting for transfers between devices: 140 us -> 184 us
  other arithmetic: 42.5 us -> 2.61 us
  blocking collectives: 205 us -> 166 us
  local copies, waits for them, and re-layouts: 42.9 us -> 7.92 us
  between operations: 2.17 us -> 15.5 us
  matrix products: 19.1 us -> 30.4 us
    all_to_all x1, blocking collectives: 162 us -> 76.3 us  [shards(): lax.all_to_all(send, ('x', 'core'), split_axis=0, concat_axis=0, tiled=True)]
    all_to_all x1, waiting for transfers between devices: 140 us -> 71.3 us  [shards(): lax.all_to_all(result.reshape(recv.shape), ('x', 'core'), split_axis=0, c...]
    all_gather x0 -> x1, waiting for transfers between devices: none -> 61 us  [shards(): held = lax.all_gather(packed, 'z')]
    reduce_scatter x0 -> x1, waiting for transfers between devices: none -> 51.8 us  [shards(): lax.psum_scatter(part.astype(jnp.bfloat16), 'z', scatter_dimension=0, til...]
    all_gather x4 -> x1, blocking collectives: 42.5 us -> 89.8 us  [shards(): pairs = lax.all_gather(pair, EP_DP, tiled=True)]
    another operation x3 -> x0, other arithmetic: 31.3 us -> none
    scatter x2 -> x0, local copies, waits for them, and re-layouts: 18.2 us -> none  [the longest x1 10.7 us: shards(): jnp.zeros((experts * capacity, width), jnp.bfloat16).at[destination]]
    gather x1 -> x0, local copies, waits for them, and re-layouts: 12.4 us -> none  [shards(): returned_flat[destination].astype(jnp.float32).reshape(tok_dev, TOP, width)]
  transfers between devices with their start and end apart: 1 -> 3, of which waited for: 1 -> 3; matrix products, arithmetic and copies ran while one was open for 0% -> 0% of each run, Pallas kernels for 0% -> 0%
where the time goes in v1:
time: 413 us; the launch traced here: 412 us
  waiting for transfers between devices  184 us (45%)
  blocking collectives  166 us (40%)
  matrix products  30.4 us (7%)
  between operations  15.5 us (4%)
  local copies, waits for them, and re-layouts  7.92 us (2%)
  starting transfers between devices  5.71 us (1%)
    all_gather x1, blocking collectives, shards(): pairs = lax.all_gather(pair, EP_DP, tiled=True)  89.8 us
    all_to_all x1, blocking collectives, shards(): lax.all_to_all(send, ('x', 'core'), split_axis=0, concat_axis=0, tiled=True)  76.3 us
    all_to_all x1, waiting for transfers between devices, shards(): lax.all_to_all(result.reshape(recv.shape), ('x', 'core'), split_axis=0, c...  71.3 us
    all_gather x1, waiting for transfers between devices, shards(): held = lax.all_gather(packed, 'z')  61 us
    reduce_scatter x1, waiting for transfers between devices, shards(): lax.psum_scatter(part.astype(jnp.bfloat16), 'z', scatter_dimension=0, til...  51.8 us
  transfers between devices with their start and end apart: 3, of which 3 were waited for; matrix products, arithmetic and copies ran while one was open for 0% of the time, Pallas kernels for 0%

profile of v1, /device:TPU:1, one launch (start us, length us, event | category | flops | bytes accessed | tf_op | source)
XLA Modules:
  0.0 412.3 jit_solution(16684683082836953582)
XLA Ops:
  7.2 0.0 copy-start
  7.2 0.0 all-gather.4.cloned.1.call-start
  7.2 0.9 fusion.14
  8.1 0.2 fusion.10
  8.3 0.1 copy.31
  8.5 0.7 fusion.19
  9.2 0.1 copy.32
  9.3 1.9 concatenate.3
  11.2 0.0 all-gather.4.cloned.1.call-update
  11.2 61.0 %all-gather.4.cloned.1.call-done = bf16[1024,2176]{1,0:T(8,128)(2,1)} async-done(((bf16[128,2176]{1,0:T(8,128)(2,1)}), bf16[1024,2176]{1,0:T(8,128)(2,1)}) %all-gather.4.cloned.1.call-update) | async-done | bytes 4456464 | tf_op jit(solution)/shard_map/all_gather | solution.py:27
  72.2 1.8 fusion.29
  74.0 1.1 copy.33
  75.1 0.8 copy.35
  75.9 0.7 constant_dynamic-slice_fusion
  76.6 4.0 fusion.3
  80.6 1.1 copy.37
  81.7 0.0 copy-start.2
  81.7 76.3 %all_to_all.10 = bf16[8,192,2048]{2,1,0:T(8,128)(2,1)S(1)} all-to-all(bf16[8,192,2048]{2,1,0:T(8,128)(2,1)S(1)} %bitcast.54), channel_id=1, replica_groups=mesh['x'=4,'z'=8,'core'=2,'dp'=4] {'x','core'}, dimensions={0} | all-to-all | bytes 12582912 | tf_op jit(solution)/shard_map/all_to_all | solution.py:41
  158.0 0.0 copy-done.2
  158.0 0.0 copy-start.3
  158.0 5.2 %fusion.8 = f32[1536,768]{1,0:T(8,128)S(1)} fusion(bf16[1536,2048]{1,0:T(8,128)(2,1)S(1)} %bitcast.56, bf16[1,2048,768]{2,1,0:T(8,128)(2,1)S(1)} %copy-done.2), kind=kOutput, calls=%fused_computation.10 | convolution fusion | flops 4831838208 | bytes 14155776 | tf_op jit(solution)/shard_map/dot_general | solution.py:43
  163.2 0.0 copy-done.3
  163.2 5.6 %multiply_convert_fusion = bf16[1536,768]{1,0:T(8,128)(2,1)S(1)} fusion(f32[1536,768]{1,0:T(8,128)S(1)} %fusion.8, bf16[1536,2048]{1,0:T(8,128)(2,1)S(1)} %bitcast.57, bf16[1,2048,768]{2,1,0:T(8,128)(2,1)S(1)} %copy-done.3), kind=kOutput, calls=%fused_computation.4 | convolution fusion | flops 4838916096 | bytes 16515072 | tf_op jit(solution)/shard_map/dot_general | solution.py:44
  168.9 0.0 copy-done
  168.9 7.0 %convolution_convert_fusion = bf16[1536,2048]{1,0:T(8,128)(2,1)} fusion(bf16[1536,768]{1,0:T(8,128)(2,1)S(1)} %multiply_convert_fusion, bf16[1,768,2048]{2,1,0:T(8,128)(2,1)S(1)} %copy-done), kind=kOutput, calls=%fused_computation.1 | convolution fusion | flops 4834983936 | bytes 11796480 | tf_op jit(solution)/shard_map/dot_general | solution.py:46
  175.9 5.7 %all-to-all-start.1 = ((bf16[8,192,2048]{2,1,0:T(8,128)(2,1)}), bf16[8,192,2048]{2,1,0:T(8,128)(2,1)}, u32[]{:S(2)}, u32[]{:S(2)}) async-start(bf16[8,192,2048]{2,1,0:T(8,128)(2,1)} %bitcast.55), calls=%async_computation.1 | async-start | bytes 12582912 | tf_op jit(solution)/shard_map/all_to_all | solution.py:47
  181.6 0.0 reduce-scatter.2.cloned.1.call-start
  181.6 71.3 %all-to-all-done.1 = bf16[8,192,2048]{2,1,0:T(8,128)(2,1)} async-done(((bf16[8,192,2048]{2,1,0:T(8,128)(2,1)}), bf16[8,192,2048]{2,1,0:T(8,128)(2,1)}, u32[]{:S(2)}, u32[]{:S(2)}) %all-to-all-start.1) | async-done | bytes 6291488 | tf_op jit(solution)/shard_map/all_to_all | solution.py:47
  252.8 0.0 copy-start.1
  252.8 6.1 %bitcast_convert_fusion = bf16[8,128,2048]{2,1,0:T(8,128)(2,1)} fusion(bf16[8,8,24,2048]{3,2,1,0:T(8,128)(2,1)} %bitcast.16, bf16[8,8,128]{2,0,1:T(8,128)(2,1)S(1)} %copy.36, bf16[8,8,128]{2,0,1:T(8,128)(2,1)S(1)} %copy.34), kind=kOutput, calls=%fused_computation | convolution fusion | flops 808189952 | bytes 10518528 | tf_op jit(solution)/shard_map/dslt,dslf->stf/dot_general | solution.py:51
  259.0 0.0 reduce-scatter.2.cloned.1.call-update
  259.6 51.8 %reduce-scatter.2.cloned.1.call-done = bf16[1,128,2048]{2,1,0:T(8,128)(2,1)} async-done(((bf16[8,128,2048]{2,1,0:T(8,128)(2,1)}), bf16[1,128,2048]{2,1,0:T(8,128)(2,1)}) %reduce-scatter.2.cloned.1.call-update) | async-done | bytes 524304 | tf_op jit(solution)/shard_map/reduce_scatter | solution.py:52
  311.5 0.0 copy-done.1
  311.5 2.2 fusion.11
  314.4 0.1 maximum_bitcast_fusion
  314.5 89.8 %all-gather.1 = f32[256,1,2]{2,1,0:T(1,128)S(1)} all-gather(f32[1,1,2]{2,1,0:T(1,128)S(1)} %maximum_bitcast_fusion), channel_id=1, replica_groups=mesh['x'=4,'z'=8,'core'=2,'dp'=4] {'x','z','core','dp'}, dimensions={0}, use_global_device_ids=true | all-gather | bytes 2056 | tf_op jit(solution)/shard_map/all_gather | solution.py:57
  404.3 0.2 slice_reduce_fusion.1
  404.5 0.1 select_reduce_fusion.2
  404.7 0.2 select_reduce_fusion.3
  404.8 0.6 pad_maximum_fusion
  (3 shorter events, 0.0 us)
Async XLA Ops:
  7.2 161.7 %copy-start = (bf16[1,768,2048]{2,1,0:T(8,128)(2,1)S(1)}, bf16[1,768,2048]{2,1,0:T(8,128)(2,1)}, u32[]{:S(2)}) copy-start(bf16[1,768,2048]{2,1,0:T(8,128)(2,1)} %param.13) | copy-start | bytes 9437188
  7.2 65.0 %all-gather.4.cloned.1.call-start = ((), (), s32[]{:S(2)}) async-start(), calls=%async_computation.4 | async-start | bytes 5013504 | tf_op jit(solution)/shard_map/all_gather | solution.py:27
  81.7 76.3 %copy-start.2 = (bf16[1,2048,768]{2,1,0:T(8,128)(2,1)S(1)}, bf16[1,2048,768]{2,1,0:T(8,128)(2,1)}, u32[]{:S(2)}) copy-start(bf16[1,2048,768]{2,1,0:T(8,128)(2,1)} %param.11) | copy-start | bytes 9437188
  158.0 5.2 %copy-start.3 = (bf16[1,2048,768]{2,1,0:T(8,128)(2,1)S(1)}, bf16[1,2048,768]{2,1,0:T(8,128)(2,1)}, u32[]{:S(2)}) copy-start(bf16[1,2048,768]{2,1,0:T(8,128)(2,1)} %param.12) | copy-start | bytes 9437188
  175.9 76.9 %all-to-all-start.1 = ((bf16[8,192,2048]{2,1,0:T(8,128)(2,1)}), bf16[8,192,2048]{2,1,0:T(8,128)(2,1)}, u32[]{:S(2)}, u32[]{:S(2)}) async-start(bf16[8,192,2048]{2,1,0:T(8,128)(2,1)} %bitcast.55), calls=%async_computation.1 | async-start | bytes 12582912 | tf_op jit(solution)/shard_map/all_to_all | solution.py:47
  181.6 129.9 %reduce-scatter.2.cloned.1.call-start = ((), (), s32[]{:S(2)}) async-start(), calls=%async_computation.3 | async-start | bytes 4718592 | tf_op jit(solution)/shard_map/reduce_scatter | solution.py:52
  252.8 58.6 %copy-start.1 = (f32[2048]{0:T(1024)S(1)}, f32[2048]{0:T(1024)}, u32[]{:S(2)}) copy-start(f32[2048]{0:T(1024)} %param.14) | copy-start | bytes 24580
Sparse Core Ops, SparseCore 0:
  11.3 60.8 all-gather.3
  259.1 52.2 reduce-scatter.1
